TPU v7x, 32 devices: a whole 2x2x4 slice. The times are simulated.
32 devices in a mesh: role: 2 (over x), grp: 8 (over z, y), tp: 2 (over core).
Axes of the slice: x: 2, y: 2, z: 4, core: 2. Of those that a mesh axis runs over, the one named last changes fastest.
Arguments:
- q_new: bfloat16 [256, 4096], P('grp', ('role', 'tp')), may hold values from -9 to 9
- k_new: bfloat16 [256, 512], P('grp', ('role', 'tp')), may hold values from -6 to 6
- v_new: bfloat16 [256, 512], P('grp', ('role', 'tp')), may hold values from -6 to 6
- k_cache: bfloat16 [256, 128, 512], P('grp', None, ('role', 'tp')), may hold values from -9 to 9
- v_cache: bfloat16 [256, 128, 512], P('grp', None, ('role', 'tp')), may hold values from -6 to 6
- cache_len: int32 [256], P('grp'), may hold values from 1 to 127
- cycle_start: int32 [256], P('grp'), may hold values from 0 to 127
- residual: bfloat16 [256, 2880], P('grp', ('role', 'tp')), may hold values from -6 to 6
- out_proj: bfloat16 [4096, 2880], P(('role', 'tp')), may hold values from -0.09375 to 0.09375
- norm_gain: float32 [2880], replicated, may hold values from 0.25 to 1.75
- router: bfloat16 [2880, 8], P(('role', 'tp')), may hold values from -0.21875 to 0.21875
- route_ids: int32 [256, 4], P('grp'), may hold values from 0 to 7, all different within a row; in each aligned block of 32 rows (0 to 31, 32 to 63, ...) at most 18 rows name the same one
- w_gate: bfloat16 [8, 2880, 1440], P('grp', None, ('role', 'tp')), may hold values from -0.109375 to 0.109375
- w_up: bfloat16 [8, 2880, 1440], P('grp', None, ('role', 'tp')), may hold values from -0.109375 to 0.109375
- w_down: bfloat16 [8, 1440, 2880], P('grp', ('role', 'tp')), may hold values from -0.15625 to 0.15625
Outputs:
- attended: bfloat16 [256, 2880], P('grp', ('role', 'tp'))
- expert_mix: bfloat16 [256, 2880], P('grp', ('role', 'tp'))
Inputs may be any that keep to these rules, and one draw needn't show every extreme that they name: `route_ids`: the 4 experts of a token differ. Among the tokens of one grp index (aligned blocks of 32 tokens) no expert is named more than 18 times, a bound that some block reaches.
All inputs are finite; a program needn't handle non-finite values.
Results may differ from a plain program's by a relative error of at most 0.017.
Values may be sent and summed in bfloat16 or wider, within the bound.
No kernel may reach another device: no remote copies, remote signals or barrier semaphores. Data moves between devices by JAX's collectives and lax.ppermute only.
A program may use at most 64 MiB of HBM per device.

v0:
```python
import functools
import math

import jax
import jax.numpy as jnp
import numpy as np
from jax import lax
from jax.experimental import pallas as pl
from jax.experimental.pallas import tpu as pltpu
from jax.sharding import PartitionSpec as P


HEADS = 64
KV_HEADS = 8
HD = 64


epsilon = 1e-05
COVER = 1 << 33


def attend_kernel(
    len_hbm, start_hbm, q_hbm, kn_hbm, vn_hbm, k_hbm, v_hbm, wo_hbm,
    *rest, grouped, chunks, parts, n_tp,
):
    share = lax.axis_index("role") * n_tp + lax.axis_index("tp")
    early = parts // 2
    outs, (stacked_ref, later_ref), rest = rest[:early], rest[early : early + 2], rest[early + 2 :]
    len_ref, start_ref, q_ref, kn_ref, vn_ref, kbuf, vbuf, wobuf = rest[:8]
    queries, heads, scores, products, small, ksem, vsem, wsem = rest[8:]
    tokens, window, lanes = k_hbm.shape
    pairs = (
        (q_hbm, q_ref), (kn_hbm, kn_ref), (vn_hbm, vn_ref), (len_hbm, len_ref),
        (start_hbm, start_ref),
    )
    firsts = [pltpu.make_async_copy(a, b, small.at[n]) for n, (a, b) in enumerate(pairs)]
    for copy in firsts:
        copy.start()
    n_heads = q_ref.shape[1] // HD
    step = tokens // chunks
    rows = wo_hbm.shape[0] // parts

    def kcopy(n):
        at = pl.ds(n * step, step)
        return pltpu.make_async_copy(k_hbm.at[at], kbuf.at[at], ksem.at[n])

    def vcopy(n):
        at = pl.ds(n * step, step)
        return pltpu.make_async_copy(v_hbm.at[at], vbuf.at[at], vsem.at[n])

    def wrows(k):
        return pl.ds(pl.multiple_of((share ^ k) * rows, 16), rows)

    def wcopy(k):
        target = wobuf.at[k - early] if k >= early else later_ref.at[k]
        return pltpu.make_async_copy(wo_hbm.at[wrows(k)], target, wsem.at[k])

    for n in range(chunks):
        kcopy(n).start()
        vcopy(n).start()
    for k in reversed(range(early, parts)):
        wcopy(k).start()
    for copy in firsts:
        copy.wait()
    lane = lax.broadcasted_iota(jnp.int32, (tokens, lanes), 1)
    per = lanes // HD

    def shifted(x, source, target):
        if source == target:
            return x
        return pltpu.roll(x, ((target - source) * HD) % lanes, 1)

    for h in range(n_heads):
        at = h // per * lanes
        x = q_ref[:, at : at + lanes].astype(jnp.float32)
        kv = h // grouped
        x = jnp.where(lane // HD == kv, shifted(x, h % per, kv), 0.0)
        queries[h * tokens : (h + 1) * tokens, :] = x
    factor = HD ** (-0.5)
    slots = lax.broadcasted_iota(jnp.int32, (1, window), 1)
    own_keys = kn_ref[...].astype(jnp.float32)
    own_values = vn_ref[...].astype(jnp.float32)
    block = step * n_heads
    for n in range(chunks):
        kcopy(n).wait()
        if n == 0:
            for k in reversed(range(early)):
                wcopy(k).start()
        for t in range(n * step, (n + 1) * step):
            query = queries[pl.ds(t, n_heads, stride=tokens), :]
            dots = lax.dot_general(
                query.astype(jnp.bfloat16), kbuf[t], (((1,), (1,)), ((), ())),
                preferred_element_type=jnp.float32,
            )
            age = slots - start_ref[t]
            age = jnp.where(age < 0, age + window, age)
            at = pl.ds(t * n_heads, n_heads)
            scores[at, :] = jnp.where(age < len_ref[t], factor * dots, -1e30)
            products[at, :] = query * own_keys[t : t + 1, :]
    for n in range(chunks):
        at = pl.ds(n * block, block)
        masked = scores[at, :]
        own = factor * jnp.sum(products[at, :], axis=1, keepdims=True)
        highest = jnp.maximum(jnp.max(masked, axis=1, keepdims=True), own)
        lifted = jnp.exp(masked - highest)
        own_lift = jnp.exp(own - highest)
        denominator = jnp.sum(lifted, axis=1, keepdims=True) + own_lift
        weights = (lifted / denominator).astype(jnp.bfloat16)
        own_weight = (own_lift / denominator).astype(jnp.bfloat16).astype(jnp.float32)
        vcopy(n).wait()
        for m in range(step):
            t = n * step + m
            mine = slice(m * n_heads, (m + 1) * n_heads)
            mixed = jnp.dot(weights[mine], vbuf[t], preferred_element_type=jnp.float32)
            mixed = mixed + own_weight[mine] * own_values[t : t + 1, :]
            heads[pl.ds(t, n_heads, stride=tokens), :] = mixed
    columns = []
    for c in range(n_heads // per):
        column = None
        for p in range(per):
            h = c * per + p
            x = shifted(heads[h * tokens : (h + 1) * tokens, :], h // grouped, p)
            column = x if column is None else jnp.where(lane // HD == p, x, column)
        columns.append(column.astype(jnp.bfloat16))
    stacked = jnp.concatenate(columns, axis=1)
    stacked_ref[...] = stacked
    for k in reversed(range(early, parts)):
        wcopy(k).wait()
        piece = lax.dot_general(
            stacked, wobuf[k - early], (((1,), (1,)), ((), ())),
            preferred_element_type=jnp.float32,
        )
        outs[k - early][...] = piece.astype(outs[k - early].dtype)
    for k in reversed(range(early)):
        wcopy(k).wait()


def project_kernel(stacked_ref, later_ref, *outs):
    for k in reversed(range(len(outs))):
        piece = lax.dot_general(
            stacked_ref[...], later_ref[k], (((1,), (1,)), ((), ())),
            preferred_element_type=jnp.float32,
        )
        outs[k][...] = piece.astype(outs[k].dtype)


def attend_project(
    q_new, k_new, v_new, k_cache, v_cache, cache_len, cycle_start, out_proj, parts, n_tp
):
    tokens, window, lanes = k_cache.shape
    n_heads = q_new.shape[1] // HD
    quarter = out_proj.shape[0] // parts
    chunks = 2
    vmem = pl.BlockSpec(memory_space=pltpu.VMEM)
    hbm = pl.BlockSpec(memory_space=pltpu.HBM)
    inputs = [
        pltpu.with_memory_space_constraint(x, pltpu.HBM)
        for x in (
            cache_len, cycle_start, q_new, k_new, v_new, k_cache, v_cache, out_proj
        )
    ]
    early = parts // 2
    piece = jax.ShapeDtypeStruct((tokens, quarter), jnp.bfloat16)
    made = pl.pallas_call(
        functools.partial(
            attend_kernel, grouped=HEADS // KV_HEADS, chunks=chunks, parts=parts, n_tp=n_tp
        ),
        in_specs=[hbm] * 8,
        out_specs=[vmem] * (early + 2),
        out_shape=[piece] * early
        + [
            jax.ShapeDtypeStruct(q_new.shape, jnp.bfloat16),
            jax.ShapeDtypeStruct((parts - early, quarter, q_new.shape[1]), out_proj.dtype),
        ],
        scratch_shapes=[
            pltpu.SMEM(cache_len.shape, jnp.int32),
            pltpu.SMEM(cycle_start.shape, jnp.int32),
            pltpu.VMEM(q_new.shape, q_new.dtype),
            pltpu.VMEM(k_new.shape, k_new.dtype),
            pltpu.VMEM(v_new.shape, v_new.dtype),
            pltpu.VMEM(k_cache.shape, k_cache.dtype),
            pltpu.VMEM(v_cache.shape, v_cache.dtype),
            pltpu.VMEM((parts - early, quarter, q_new.shape[1]), out_proj.dtype),
            pltpu.VMEM((n_heads * tokens, lanes), jnp.float32),
            pltpu.VMEM((n_heads * tokens, lanes), jnp.float32),
            pltpu.VMEM((n_heads * tokens, window), jnp.float32),
            pltpu.VMEM((n_heads * tokens, lanes), jnp.float32),
            pltpu.SemaphoreType.DMA((5,)),
            pltpu.SemaphoreType.DMA((chunks,)),
            pltpu.SemaphoreType.DMA((chunks,)),
            pltpu.SemaphoreType.DMA((parts,)),
        ],
        compiler_params=pltpu.CompilerParams(vmem_limit_bytes=16 << 20),
        name="attend_project",
    )(*inputs)
    first, (stacked, later) = made[:early], made[early:]
    later_call = pl.pallas_call(
        project_kernel,
        in_specs=[vmem, vmem],
        out_specs=[vmem] * early,
        out_shape=[jax.ShapeDtypeStruct((tokens, quarter), jnp.float32)] + [piece] * (early - 1),
        compiler_params=pltpu.CompilerParams(vmem_limit_bytes=8 << 20),
        name="project",
    )
    rest = later_call(stacked, later)
    return list(rest) + list(first)


def for_each_core(n_role, n_tp, body):
    role = lax.axis_index("role")
    slots = [role ^ r for r in range(n_role)]
    for tp in range(n_tp):
        places = [r * n_tp + tp for r in range(n_role)]
        pairs = [r * n_tp + (tp ^ 1) for r in range(n_role)]
        pl.when(lax.axis_index("tp") == tp)(functools.partial(body, slots, places, pairs))


def window_of(place, quarter):
    first, last = place * quarter, (place + 1) * quarter
    start = first // 128 * 128
    return slice(start, last), first - start


def partial_products(refs, places, gate_ref, up_ref, quarter):
    turned = (((1,), (1,)), ((), ()))
    gate_lin = up_lin = 0.0
    for x, p in zip(refs, places):
        at, shift = window_of(p, quarter)
        x = x[:, :quarter]
        if shift:
            x = jnp.concatenate([jnp.zeros((x.shape[0], shift), x.dtype), x], axis=1)
        gate_lin = gate_lin + lax.dot_general(
            x, gate_ref[0, :, at], turned, preferred_element_type=jnp.float32
        )
        up_lin = up_lin + lax.dot_general(
            x, up_ref[0, :, at], turned, preferred_element_type=jnp.float32
        )
    return gate_lin, up_lin


def down_products(activated, place, down_ref, quarter):
    at, shift = window_of(place, quarter)
    result = jnp.dot(activated, down_ref[0, :, at], preferred_element_type=jnp.float32)
    return result[:, shift:].astype(jnp.bfloat16)


def first_kernel(own_ref, gate_ref, up_ref, gate_out, up_out, *, quarter, n_tp):
    n_role = own_ref.shape[0]

    def body(slots, places, pairs):
        gate_out[...], up_out[...] = partial_products(
            [own_ref[i] for i in slots], places, gate_ref, up_ref, quarter
        )

    for_each_core(n_role, n_tp, body)


def second_kernel(
    own_ref, other_ref, gate_in, up_in, gate_ref, up_ref, down_ref, send_ref,
    activated_ref, *, quarter, topk, n_tp,
):
    def body(slots, places, pairs):
        second_body(
            slots, pairs, own_ref, other_ref, gate_in, up_in, gate_ref, up_ref, down_ref,
            send_ref, activated_ref, quarter, topk,
        )

    for_each_core(own_ref.shape[0], n_tp, body)


def second_body(
    slots, pairs, own_ref, other_ref, gate_in, up_in, gate_ref, up_ref, down_ref,
    send_ref, activated_ref, quarter, topk,
):
    n_role, _, _ = own_ref.shape
    tail_at = quarter // 128 * 128
    first = quarter - tail_at
    gate_lin, up_lin = partial_products(
        [other_ref[i] for i in slots], pairs, gate_ref, up_ref, quarter
    )
    tail = 0.0
    for ref in (own_ref, other_ref):
        for i in range(n_role):
            tail = tail + ref[i, :, tail_at:].astype(jnp.float32)
    ids = pltpu.roll(own_ref[0, :, tail_at:].astype(jnp.float32), topk + 1, 1)
    n_stat = 1 + topk
    span = tail.shape[1]
    tail = tail + pltpu.roll(tail, span - n_stat, 1) + pltpu.roll(tail, span - 2 * n_stat, 1)
    at = first + topk
    scale = lax.rsqrt(tail[:, at : at + 1] / down_ref.shape[2] + epsilon)
    lane = lax.broadcasted_iota(jnp.int32, tail.shape, 1)
    chosen = (lane > at) & (lane <= at + topk)
    picked = jnp.where(chosen, tail * scale, -1e30)
    lifted = jnp.exp(picked - jnp.max(picked, axis=1, keepdims=True))
    expert = lax.axis_index("grp").astype(jnp.float32)
    mine = jnp.where(chosen & (ids == expert), lifted, 0.0)
    weight = jnp.sum(mine, axis=1, keepdims=True) / jnp.sum(lifted, axis=1, keepdims=True)
    gate_lin = (gate_lin + gate_in[...]) * scale
    up_lin = (up_lin + up_in[...]) * scale
    activated = gate_lin * jax.nn.sigmoid(1.702 * gate_lin) * (up_lin + 1.0)
    activated = (activated * weight).astype(jnp.bfloat16)
    activated_ref[...] = activated
    for i, p in zip(slots, pairs):
        send_ref[i] = down_products(activated, p, down_ref, quarter)


def third_kernel(activated_ref, down_ref, keep_ref, *, quarter, n_tp):
    n_role = keep_ref.shape[0]

    def body(slots, places, pairs):
        for i, p in zip(slots, places):
            keep_ref[i] = down_products(activated_ref[...], p, down_ref, quarter)

    for_each_core(n_role, n_tp, body)


def run_first(own, w_gate, w_up, quarter, n_tp):
    vmem = pl.BlockSpec(memory_space=pltpu.VMEM)
    partial = jax.ShapeDtypeStruct((own.shape[1], w_gate.shape[1]), jnp.float32)
    return pl.pallas_call(
        functools.partial(first_kernel, quarter=quarter, n_tp=n_tp),
        in_specs=[vmem] * 3,
        out_specs=[vmem, vmem],
        out_shape=[partial, partial],
        compiler_params=pltpu.CompilerParams(vmem_limit_bytes=16 << 20),
        name="expert_first",
    )(own, w_gate, w_up)


def run_second(own, other, partials, w_gate, w_up, w_down, quarter, topk, n_tp):
    n_role, items, _ = own.shape
    vmem = pl.BlockSpec(memory_space=pltpu.VMEM)
    return pl.pallas_call(
        functools.partial(second_kernel, quarter=quarter, topk=topk, n_tp=n_tp),
        in_specs=[vmem] * 7,
        out_specs=[vmem] * 2,
        out_shape=[
            jax.ShapeDtypeStruct((n_role, items, quarter), jnp.bfloat16),
            jax.ShapeDtypeStruct((items, w_gate.shape[1]), jnp.bfloat16),
        ],
        compiler_params=pltpu.CompilerParams(vmem_limit_bytes=24 << 20),
        name="expert_second",
    )(own, other, *partials, w_gate, w_up, w_down)


def run_third(activated, w_down, n_role, quarter, n_tp):
    vmem = pl.BlockSpec(memory_space=pltpu.VMEM)
    items = activated.shape[0]
    return pl.pallas_call(
        functools.partial(third_kernel, quarter=quarter, n_tp=n_tp),
        in_specs=[vmem] * 2,
        out_specs=vmem,
        out_shape=jax.ShapeDtypeStruct((n_role, items, quarter), jnp.bfloat16),
        compiler_params=pltpu.CompilerParams(vmem_limit_bytes=12 << 20),
        name="expert_third",
    )(activated, w_down)


def three_parts(x):
    high = x.astype(jnp.bfloat16).astype(jnp.float32)
    rest = x - high
    middle = rest.astype(jnp.bfloat16).astype(jnp.float32)
    return high, middle, rest - middle


def pack_kernel(own_ref, *rest, moved):
    arrived, rest = rest[:moved], rest[moved:]
    residual_ref, gain_ref, router_ref, ids_ref, stream_ref, packed_ref = rest
    stream = residual_ref[...].astype(jnp.float32) + own_ref[...]
    for ref in arrived:
        stream = stream + ref[...].astype(jnp.float32)
    stream_ref[...] = stream
    tokens, quarter = stream.shape
    topk = ids_ref.shape[0]
    scaled = (stream * gain_ref[...]).astype(jnp.bfloat16)
    squares = jnp.sum(stream * stream, axis=1, keepdims=True)
    logits = lax.dot_general(
        scaled, router_ref[...], (((1,), (1,)), ((), ())), preferred_element_type=jnp.float32
    )
    names = lax.broadcasted_iota(jnp.int32, logits.shape, 1).astype(jnp.float32)
    eye = (
        lax.broadcasted_iota(jnp.int32, (topk, topk), 0)
        == lax.broadcasted_iota(jnp.int32, (topk, topk), 1)
    )
    ids = lax.dot_general(
        ids_ref[...].astype(jnp.float32).astype(jnp.bfloat16), eye.astype(jnp.bfloat16),
        (((0,), (0,)), ((), ())), preferred_element_type=jnp.float32,
    )
    stats = [squares]
    columns = []
    for k in range(topk):
        chosen = ids[:, k : k + 1]
        columns.append(chosen)
        stats.append(jnp.sum(jnp.where(names == chosen, logits, 0.0), axis=1, keepdims=True))
    split = [three_parts(x) for x in stats]
    for p in range(3):
        columns.extend(x[p] for x in split)
    tail_at = quarter // 128 * 128
    first = quarter - tail_at
    packed_ref[:, :quarter] = scaled
    tile = packed_ref[:, tail_at : tail_at + 128]
    lane = lax.broadcasted_iota(jnp.int32, (tokens, 128), 1)
    tail = jnp.zeros((tokens, 128), jnp.float32)
    for c, x in enumerate(columns):
        tail = jnp.where(lane == first + c, x, tail)
    packed_ref[:, tail_at : tail_at + 128] = jnp.where(
        lane < first, tile.astype(jnp.float32), tail
    ).astype(jnp.bfloat16)


def run_pack(own, arrived, residual, gain, router, route_ids):
    tokens, quarter = residual.shape
    vmem = pl.BlockSpec(memory_space=pltpu.VMEM)
    lanes = quarter // 128 * 128 + 128
    assert quarter % 128 + 4 * route_ids.shape[0] + 3 <= 128
    return pl.pallas_call(
        functools.partial(pack_kernel, moved=len(arrived)),
        in_specs=[vmem] * (5 + len(arrived)),
        out_specs=[vmem, vmem],
        out_shape=[
            jax.ShapeDtypeStruct((tokens, quarter), jnp.float32),
            jax.ShapeDtypeStruct((tokens, lanes), jnp.bfloat16),
        ],
        compiler_params=pltpu.CompilerParams(vmem_limit_bytes=4 << 20),
        cost_estimate=pl.CostEstimate(flops=COVER, transcendentals=0, bytes_accessed=1 << 20),
        name="pack",
    )(own, *arrived, residual, gain, router, route_ids)


def select_kernel(*rest, n_far, n_near, cap, topk, quarter):
    blocks, rest = rest[:n_far], rest[n_far:]
    rows, picks = rest[:n_near], rest[n_near:]
    tokens, _ = blocks[0].shape
    tail_at = quarter // 128 * 128
    first = quarter - tail_at
    stacked = jnp.concatenate([ref[...] for ref in blocks], axis=0)
    ids = stacked[:, tail_at:].astype(jnp.float32).T
    n_all = n_far * tokens
    source = lax.broadcasted_iota(jnp.int32, (n_all, n_all), 0)
    target = lax.broadcasted_iota(jnp.int32, (n_all, n_all), 1)
    same = source // tokens == target // tokens
    before = jnp.where(same & (source < target), 1.0, 0.0).astype(jnp.bfloat16)
    slot = lax.broadcasted_iota(jnp.int32, (n_far * cap, n_all), 0).astype(jnp.float32)
    base = lax.broadcasted_iota(jnp.int32, (1, n_all), 1) // tokens * cap
    hits = []
    for j in range(n_near):
        grp = lax.axis_index("grp")
        expert = (grp // n_near * n_near + (grp % n_near ^ j)).astype(jnp.float32)
        hit = jnp.zeros((1, n_all), jnp.float32)
        for k in range(topk):
            hit = hit + jnp.where(ids[first + k : first + k + 1, :] == expert, 1.0, 0.0)
        hits.append(hit)
    line = lax.broadcasted_iota(jnp.int32, (8, n_all), 0)
    table = jnp.zeros((8, n_all), jnp.float32)
    for j in range(n_near):
        table = jnp.where(line == j, hits[j], table)
    ranks = jnp.dot(table.astype(jnp.bfloat16), before, preferred_element_type=jnp.float32)
    chosen = []
    for j in range(n_near):
        at = jnp.where(hits[j] > 0.0, ranks[j : j + 1, :] + base.astype(jnp.float32), -1.0)
        pick = jnp.where(at == slot, 1.0, 0.0).astype(jnp.bfloat16)
        picks[j][...] = pick
        chosen.append(pick)
    result = jnp.dot(
        jnp.concatenate(chosen, axis=0), stacked, preferred_element_type=jnp.float32
    ).astype(jnp.bfloat16)
    for j in range(n_near):
        rows[j][...] = result[j * n_far * cap : (j + 1) * n_far * cap]


def run_select(blocks, n_near, cap, topk, quarter):
    tokens, lanes = blocks[0].shape
    n_far = len(blocks)
    vmem = pl.BlockSpec(memory_space=pltpu.VMEM)
    outs = [jax.ShapeDtypeStruct((n_far * cap, lanes), jnp.bfloat16)] * n_near
    outs += [jax.ShapeDtypeStruct((n_far * cap, n_far * tokens), jnp.bfloat16)] * n_near
    made = pl.pallas_call(
        functools.partial(
            select_kernel, n_far=n_far, n_near=n_near, cap=cap, topk=topk, quarter=quarter
        ),
        in_specs=[vmem] * n_far,
        out_specs=[vmem] * len(outs),
        out_shape=outs,
        compiler_params=pltpu.CompilerParams(vmem_limit_bytes=12 << 20),
        name="select",
    )(*blocks)
    return made[:n_near], made[n_near:]


def spread_kernel(*refs, n_near, n_role, n_far):
    rows, refs = refs[: n_near * n_role], refs[n_near * n_role :]
    picks, outs = refs[:n_near], refs[n_near:]
    total = 0.0
    for j in range(n_near):
        row = 0.0
        for i in range(n_role):
            row = row + rows[j * n_role + i][...].astype(jnp.float32)
        total = total + lax.dot_general(
            picks[j][...], row.astype(jnp.bfloat16), (((0,), (0,)), ((), ())),
            preferred_element_type=jnp.float32,
        )
    tokens = total.shape[0] // n_far
    for n in range(n_far):
        outs[n][...] = total[n * tokens : (n + 1) * tokens].astype(outs[n].dtype)


def run_spread(rows, picks, n_role, n_far):
    n_near = len(picks)
    tokens = picks[0].shape[1] // n_far
    vmem = pl.BlockSpec(memory_space=pltpu.VMEM)
    quarter = rows[0].shape[1]
    kinds = [jnp.float32] + [jnp.bfloat16] * (n_far - 1)
    return pl.pallas_call(
        functools.partial(spread_kernel, n_near=n_near, n_role=n_role, n_far=n_far),
        in_specs=[vmem] * (len(rows) + n_near),
        out_specs=[vmem] * n_far,
        out_shape=[jax.ShapeDtypeStruct((tokens, quarter), kind) for kind in kinds],
        compiler_params=pltpu.CompilerParams(vmem_limit_bytes=12 << 20),
        name="spread",
    )(*rows, *picks)


def swap_table(mesh, grp_of, role_flip, tp_flip):
    names = mesh.axis_names
    sizes = [mesh.shape[n] for n in names]
    pairs = []
    for flat in range(math.prod(sizes)):
        at = dict(zip(names, [int(v) for v in np.unravel_index(flat, sizes)]))
        to = dict(
            role=at["role"] ^ role_flip, tp=at["tp"] ^ tp_flip, grp=grp_of(at["grp"])
        )
        pairs.append((flat, int(np.ravel_multi_index([to[n] for n in names], sizes))))
    return pairs


def make_local(mesh):
    n_role, n_grp, n_tp = (mesh.shape[n] for n in ("role", "grp", "tp"))
    n_near = 2 if n_grp % 2 == 0 else 1
    n_far = n_grp // n_near
    xor_far = n_far & (n_far - 1) == 0
    names = mesh.axis_names

    def send(x, near=0, role=0, tp=0):
        return lax.ppermute(x, names, swap_table(mesh, lambda g: g ^ near, role, tp))

    def send_far(x, k):
        def grp_of(g):
            far, near = divmod(g, n_near)
            return (far ^ k if xor_far else (far + k) % n_far) * n_near + near

        return lax.ppermute(x, names, swap_table(mesh, grp_of, 0, 0))

    def local(
        q_new, k_new, v_new, k_cache, v_cache, cache_len, cycle_start, residual,
        out_proj, norm_gain, router, route_ids, w_gate, w_up, w_down,
    ):
        role, _, tp = (lax.axis_index(n) for n in ("role", "grp", "tp"))
        tokens, quarter = residual.shape
        topk = route_ids.shape[1]
        experts = n_grp * w_gate.shape[0]
        cap = max(3, tokens * topk // experts + 2)
        share = role * n_tp + tp
        parts = n_role * n_tp
        pieces = attend_project(
            q_new, k_new, v_new, k_cache, v_cache, cache_len, cycle_start, out_proj.T, parts, n_tp
        )
        moved = []
        for k in range(1, parts):
            moved.append(send(pieces[k], role=k // n_tp, tp=k % n_tp))
        gain = lax.dynamic_slice_in_dim(norm_gain, share * quarter, quarter, 0).reshape(1, quarter)
        stream, packed = run_pack(pieces[0], moved, residual, gain, router.T, route_ids.T)
        blocks = [packed] + [send_far(packed, k) for k in range(1, n_far)]
        attended = stream.astype(jnp.bfloat16)
        rows, picks = run_select(blocks, n_near, cap, topk, quarter)
        arrived = {(0, 0): rows[0]}
        for j in range(n_near):
            for i in range(n_role):
                if (j, i) != (0, 0):
                    arrived[j, i] = send(rows[j], near=j, role=i)
        half = jnp.stack(
            [jnp.concatenate([arrived[j, i] for j in range(n_near)], 0) for i in range(n_role)]
        )
        other = send(half, tp=1)
        gate_turned, up_turned = jnp.swapaxes(w_gate, 1, 2), jnp.swapaxes(w_up, 1, 2)
        partials = run_first(half, gate_turned, up_turned, quarter, n_tp)
        sent, activated = run_second(
            half, other, partials, gate_turned, up_turned, w_down, quarter, topk, n_tp
        )
        returned = send(sent, tp=1)
        kept = run_third(activated, w_down, n_role, quarter, n_tp)
        acc = kept.astype(jnp.float32) + returned.astype(jnp.float32)
        acc = acc.astype(jnp.bfloat16).reshape(n_role, n_near, n_far * cap, quarter)
        back = []
        for j in range(n_near):
            for i in range(n_role):
                piece = acc[i, j]
                if (j, i) != (0, 0):
                    piece = send(piece, near=j, role=i)
                back.append(piece)
        spread = run_spread(back, picks, n_role, n_far)
        mix = spread[0].astype(jnp.float32)
        for k in range(1, n_far):
            mix = mix + send_far(spread[k], k if xor_far else n_far - k).astype(jnp.float32)
        return (attended, mix.astype(jnp.bfloat16))

    return local


def solution(mesh):
    placed = (
        P("grp", ("role", "tp")),
        P("grp", ("role", "tp")),
        P("grp", ("role", "tp")),
        P("grp", None, ("role", "tp")),
        P("grp", None, ("role", "tp")),
        P("grp"),
        P("grp"),
        P("grp", ("role", "tp")),
        P(("role", "tp"), None),
        P(),
        P(("role", "tp"), None),
        P("grp", None),
        P("grp", None, ("role", "tp")),
        P("grp", None, ("role", "tp")),
        P("grp", ("role", "tp"), None),
    )
    local = make_local(mesh)

    return jax.shard_map(
        local,
        mesh=mesh,
        in_specs=placed,
        out_specs=(P("grp", ("role", "tp")), P("grp", ("role", "tp"))),
        check_vma=False,
    )
```

profile of v0, /device:TPU:0, one launch (start us, length us, event | category | flops | bytes accessed | tf_op | source)
XLA Modules:
  0.0 52.7 jit_solution(9147862595422128821)
XLA Ops:
  0.6 3.9 %attend_project.1 = (bf16[32,720]{1,0:T(8,128)(2,1)S(1)}, bf16[32,720]{1,0:T(8,128)(2,1)S(1)}, bf16[32,1024]{1,0:T(8,128)(2,1)S(1)}, bf16[2,720,1024]{2,1,0:T(8,128)(2,1)S(1)}) custom-call(s32[32]{0:T(128)} %len_hbm.1, s32[32]{0:T(128)} %start_hbm.1, bf16[32,1024]{1,0:T(8,128)(2,1)} %q_hbm.1, bf16[32,128]{1,0:T(8,128)(2,1)} %kn_hbm.1, ...), custom_call_target="tpu_custom_call" | custom-call | tf_op jit(solution)/shard_map/attend_project/pallas_call | solution.py:164
  4.6 0.9 %project.1 = (f32[32,720]{1,0:T(8,128)S(1)}, bf16[32,720]{1,0:T(8,128)(2,1)S(1)}) custom-call(bf16[32,1024]{1,0:T(8,128)(2,1)S(1)} %get-tuple-element.22.stacked_ref, bf16[2,720,1024]{2,1,0:T(8,128)(2,1)S(1)} %get-tuple-element.23.later_ref), custom_call_target="tpu_custom_call" | custom-call | tf_op jit(solution)/shard_map/project/pallas_call | solution.py:205
  5.5 0.5 collective-permute-start
  6.0 2.5 %collective-permute-start.1 = (bf16[32,720]{1,0:T(8,128)(2,1)S(1)}, bf16[32,720]{1,0:T(8,128)(2,1)S(1)}, u32[]{:S(2)}, u32[]{:S(2)}) collective-permute-start(bf16[32,720]{1,0:T(8,128)(2,1)S(1)} %get-tuple-element.26), channel_id=1, source_target_pairs={{0,16},{1,17},{2,18},{3,19},{4,20},{5,21},{6,22},{7,23},{8,24},{9,... | collective-permute-start | bytes 138248 | tf_op jit(solution)/shard_map/ppermute | solution.py:544
  8.6 0.8 %dynamic_slice.3 = f32[720]{0:T(1024)S(1)} dynamic-slice(f32[2880]{0:T(1024)} %param.24, s32[]{:T(128)S(6)} %select_n.3), dynamic_slice_sizes={720} | dynamic-slice | bytes 5764 | tf_op jit(solution)/shard_map/dynamic_slice | solution.py:570
  9.4 1.5 %collective-permute-done.1.rest_1_ = bf16[32,720]{1,0:T(8,128)(2,1)S(1)} collective-permute-done((bf16[32,720]{1,0:T(8,128)(2,1)S(1)}, bf16[32,720]{1,0:T(8,128)(2,1)S(1)}, u32[]{:S(2)}, u32[]{:S(2)}) %collective-permute-start.1) | collective-permute-done | bytes 46112 | tf_op jit(solution)/shard_map/ppermute | solution.py:544
  10.9 1.4 %collective-permute-done.2.rest_2_ = bf16[32,720]{1,0:T(8,128)(2,1)S(1)} collective-permute-done((bf16[32,720]{1,0:T(8,128)(2,1)S(1)}, bf16[32,720]{1,0:T(8,128)(2,1)S(1)}, u32[]{:S(2)}, u32[]{:S(2)}) %collective-permute-start.2) | collective-permute-done | bytes 46112 | tf_op jit(solution)/shard_map/ppermute | solution.py:544
  12.7 1.6 %collective-permute-start.3 = (bf16[32,768]{1,0:T(8,128)(2,1)S(1)}, bf16[32,768]{1,0:T(8,128)(2,1)S(1)}, u32[]{:S(2)}, u32[]{:S(2)}) collective-permute-start(bf16[32,768]{1,0:T(8,128)(2,1)S(1)} %get-tuple-element.29.rest_0_), channel_id=1, source_target_pairs={{0,4},{1,5},{2,6},{3,7},{4,0},{5,1},{6,2},{7,3},{8,12},{9,13},{10,... | collective-permute-start | bytes 147464 | tf_op jit(solution)/shard_map/ppermute | solution.py:551
  14.3 2.6 %collective-permute-start.4 = (bf16[32,768]{1,0:T(8,128)(2,1)S(1)}, bf16[32,768]{1,0:T(8,128)(2,1)S(1)}, u32[]{:S(2)}, u32[]{:S(2)}) collective-permute-start(bf16[32,768]{1,0:T(8,128)(2,1)S(1)} %get-tuple-element.29.rest_0_), channel_id=1, source_target_pairs={{0,8},{1,9},{2,10},{3,11},{4,12},{5,13},{6,14},{7,15},{8,0},{9,1},... | collective-permute-start | bytes 147464 | tf_op jit(solution)/shard_map/ppermute | solution.py:551
  17.1 3.1 %collective-permute-done.4.rest_2_ = bf16[32,768]{1,0:T(8,128)(2,1)S(1)} collective-permute-done((bf16[32,768]{1,0:T(8,128)(2,1)S(1)}, bf16[32,768]{1,0:T(8,128)(2,1)S(1)}, u32[]{:S(2)}, u32[]{:S(2)}) %collective-permute-start.4) | collective-permute-done | bytes 49184 | tf_op jit(solution)/shard_map/ppermute | solution.py:551
  20.2 2.6 %collective-permute-done.5.rest_3_ = bf16[32,768]{1,0:T(8,128)(2,1)S(1)} collective-permute-done((bf16[32,768]{1,0:T(8,128)(2,1)S(1)}, bf16[32,768]{1,0:T(8,128)(2,1)S(1)}, u32[]{:S(2)}, u32[]{:S(2)}) %collective-permute-start.5) | collective-permute-done | bytes 49184 | tf_op jit(solution)/shard_map/ppermute | solution.py:551
  23.2 1.6 %collective-permute-start.6 = (bf16[72,768]{1,0:T(8,128)(2,1)S(1)}, bf16[72,768]{1,0:T(8,128)(2,1)S(1)}, u32[]{:S(2)}, u32[]{:S(2)}) collective-permute-start(bf16[72,768]{1,0:T(8,128)(2,1)S(1)} %get-tuple-element.31), channel_id=1, source_target_pairs={{0,2},{1,3},{2,0},{3,1},{4,6},{5,7},{6,4},{7,5},{8,10},{9,11},{10,... | collective-permute-start | bytes 331784 | tf_op jit(solution)/shard_map/ppermute | solution.py:544
  24.8 0.9 %collective-permute-start.8 = (bf16[72,768]{1,0:T(8,128)(2,1)S(1)}, bf16[72,768]{1,0:T(8,128)(2,1)S(1)}, u32[]{:S(2)}, u32[]{:S(2)}) collective-permute-start(bf16[72,768]{1,0:T(8,128)(2,1)S(1)} %get-tuple-element.31), channel_id=1, source_target_pairs={{0,18},{1,19},{2,16},{3,17},{4,22},{5,23},{6,20},{7,21},{8,26},{9,... | collective-permute-start | bytes 331784 | tf_op jit(solution)/shard_map/ppermute | solution.py:544
  25.7 1.1 %collective-permute-start.7 = (bf16[72,768]{1,0:T(8,128)(2,1)S(1)}, bf16[72,768]{1,0:T(8,128)(2,1)S(1)}, u32[]{:S(2)}, u32[]{:S(2)}) collective-permute-start(bf16[72,768]{1,0:T(8,128)(2,1)S(1)} %get-tuple-element.30), channel_id=1, source_target_pairs={{0,16},{1,17},{2,18},{3,19},{4,20},{5,21},{6,22},{7,23},{8,24},{9,... | collective-permute-start | bytes 331784 | tf_op jit(solution)/shard_map/ppermute | solution.py:544
  26.8 2.1 %collective-permute-done.6 = bf16[72,768]{1,0:T(8,128)(2,1)S(1)} collective-permute-done((bf16[72,768]{1,0:T(8,128)(2,1)S(1)}, bf16[72,768]{1,0:T(8,128)(2,1)S(1)}, u32[]{:S(2)}, u32[]{:S(2)}) %collective-permute-start.6) | collective-permute-done | bytes 110624 | tf_op jit(solution)/shard_map/ppermute | solution.py:544
  28.9 1.6 %collective-permute-done.8 = bf16[72,768]{1,0:T(8,128)(2,1)S(1)} collective-permute-done((bf16[72,768]{1,0:T(8,128)(2,1)S(1)}, bf16[72,768]{1,0:T(8,128)(2,1)S(1)}, u32[]{:S(2)}, u32[]{:S(2)}) %collective-permute-start.8) | collective-permute-done | bytes 110624 | tf_op jit(solution)/shard_map/ppermute | solution.py:544
  30.9 0.9 %expert_first.1 = (f32[144,360]{1,0:T(8,128)S(1)}, f32[144,360]{1,0:T(8,128)S(1)}) custom-call(bf16[2,144,768]{2,1,0:T(8,128)(2,1)S(1)} %pad_maximum_fusion.own_ref, bf16[1,360,2880]{2,1,0:T(8,128)(2,1)S(1)} %bitcast.18, bf16[1,360,2880]{2,1,0:T(8,128)(2,1)S(1)} %bitcast.20), custom_call_target="tpu_custom_call" | custom-call | tf_op jit(solution)/shard_map/expert_first/pallas_call | solution.py:320
  31.8 0.8 %collective-permute-done.9.other_ref = bf16[2,144,768]{2,1,0:T(8,128)(2,1)S(1)} collective-permute-done((bf16[2,144,768]{2,1,0:T(8,128)(2,1)S(1)}, bf16[2,144,768]{2,1,0:T(8,128)(2,1)S(1)}, u32[]{:S(2)}, u32[]{:S(2)}) %collective-permute-start.9) | collective-permute-done | bytes 442400 | tf_op jit(solution)/shard_map/ppermute | solution.py:544
  32.6 1.6 %expert_second.1 = (bf16[2,144,720]{2,1,0:T(8,128)(2,1)S(1)}, bf16[144,360]{1,0:T(8,128)(2,1)S(1)}) custom-call(bf16[2,144,768]{2,1,0:T(8,128)(2,1)S(1)} %pad_maximum_fusion.own_ref, bf16[2,144,768]{2,1,0:T(8,128)(2,1)S(1)} %collective-permute-done.9.other_ref, f32[144,360]{1,0:T(8,128)S(1)} %get-tuple-element.32.gate_in, ...), custom_call_target="tpu_custom_call" | custom-call | tf_op jit(solution)/shard_map/expert_second/pallas_call | solution.py:333
  34.9 1.2 %collective-permute-done.10 = bf16[2,144,720]{2,1,0:T(8,128)(2,1)S(1)} collective-permute-done((bf16[2,144,720]{2,1,0:T(8,128)(2,1)S(1)}, bf16[2,144,720]{2,1,0:T(8,128)(2,1)S(1)}, u32[]{:S(2)}, u32[]{:S(2)}) %collective-permute-start.10) | collective-permute-done | bytes 414752 | tf_op jit(solution)/shard_map/ppermute | solution.py:544
  36.2 1.0 %collective-permute-start.11 = (bf16[72,720]{1,0:T(8,128)(2,1)S(1)}, bf16[72,720]{1,0:T(8,128)(2,1)S(1)}, u32[]{:S(2)}, u32[]{:S(2)}) collective-permute-start(bf16[72,720]{1,0:T(8,128)(2,1)S(1)} %get-tuple-element.44), channel_id=1, source_target_pairs={{0,16},{1,17},{2,18},{3,19},{4,20},{5,21},{6,22},{7,23},{8,24},{9,... | collective-permute-start | bytes 311048 | tf_op jit(solution)/shard_map/ppermute | solution.py:544
  37.2 1.5 %collective-permute-start.12 = (bf16[72,720]{1,0:T(8,128)(2,1)S(1)}, bf16[72,720]{1,0:T(8,128)(2,1)S(1)}, u32[]{:S(2)}, u32[]{:S(2)}) collective-permute-start(bf16[72,720]{1,0:T(8,128)(2,1)S(1)} %get-tuple-element.43), channel_id=1, source_target_pairs={{0,2},{1,3},{2,0},{3,1},{4,6},{5,7},{6,4},{7,5},{8,10},{9,11},{10,... | collective-permute-start | bytes 311048 | tf_op jit(solution)/shard_map/ppermute | solution.py:544
  38.7 1.0 %collective-permute-start.13 = (bf16[72,720]{1,0:T(8,128)(2,1)S(1)}, bf16[72,720]{1,0:T(8,128)(2,1)S(1)}, u32[]{:S(2)}, u32[]{:S(2)}) collective-permute-start(bf16[72,720]{1,0:T(8,128)(2,1)S(1)} %get-tuple-element.42), channel_id=1, source_target_pairs={{0,18},{1,19},{2,16},{3,17},{4,22},{5,23},{6,20},{7,21},{8,26},{9,... | collective-permute-start | bytes 311048 | tf_op jit(solution)/shard_map/ppermute | solution.py:544
  39.8 2.1 %collective-permute-done.11.refs_1_ = bf16[72,720]{1,0:T(8,128)(2,1)S(1)} collective-permute-done((bf16[72,720]{1,0:T(8,128)(2,1)S(1)}, bf16[72,720]{1,0:T(8,128)(2,1)S(1)}, u32[]{:S(2)}, u32[]{:S(2)}) %collective-permute-start.11) | collective-permute-done | bytes 103712 | tf_op jit(solution)/shard_map/ppermute | solution.py:544
  41.9 1.5 %collective-permute-done.12.refs_2_ = bf16[72,720]{1,0:T(8,128)(2,1)S(1)} collective-permute-done((bf16[72,720]{1,0:T(8,128)(2,1)S(1)}, bf16[72,720]{1,0:T(8,128)(2,1)S(1)}, u32[]{:S(2)}, u32[]{:S(2)}) %collective-permute-start.12) | collective-permute-done | bytes 103712 | tf_op jit(solution)/shard_map/ppermute | solution.py:544
  43.5 1.2 %collective-permute-done.13.refs_3_ = bf16[72,720]{1,0:T(8,128)(2,1)S(1)} collective-permute-done((bf16[72,720]{1,0:T(8,128)(2,1)S(1)}, bf16[72,720]{1,0:T(8,128)(2,1)S(1)}, u32[]{:S(2)}, u32[]{:S(2)}) %collective-permute-start.13) | collective-permute-done | bytes 103712 | tf_op jit(solution)/shard_map/ppermute | solution.py:544
  45.0 1.1 %collective-permute-start.16 = (bf16[32,720]{1,0:T(8,128)(2,1)S(1)}, bf16[32,720]{1,0:T(8,128)(2,1)S(1)}, u32[]{:S(2)}, u32[]{:S(2)}) collective-permute-start(bf16[32,720]{1,0:T(8,128)(2,1)S(1)} %get-tuple-element.41), channel_id=1, source_target_pairs={{0,12},{1,13},{2,14},{3,15},{4,8},{5,9},{6,10},{7,11},{8,4},{9,5},... | collective-permute-start | bytes 138248 | tf_op jit(solution)/shard_map/ppermute | solution.py:551
  46.1 3.3 %collective-permute-start.14 = (bf16[32,720]{1,0:T(8,128)(2,1)S(1)}, bf16[32,720]{1,0:T(8,128)(2,1)S(1)}, u32[]{:S(2)}, u32[]{:S(2)}) collective-permute-start(bf16[32,720]{1,0:T(8,128)(2,1)S(1)} %get-tuple-element.39), channel_id=1, source_target_pairs={{0,4},{1,5},{2,6},{3,7},{4,0},{5,1},{6,2},{7,3},{8,12},{9,13},{10,... | collective-permute-start | bytes 138248 | tf_op jit(solution)/shard_map/ppermute | solution.py:551
  49.5 0.6 %convert_element_type.24 = bf16[32,720]{1,0:T(8,128)(2,1)} convert(f32[32,720]{1,0:T(8,128)S(1)} %get-tuple-element.28) | non-fusion elementwise | flops 23040 | bytes 138240 | tf_op jit(solution)/shard_map/convert_element_type | solution.py:573
  50.1 0.9 %collective-permute-done.16 = bf16[32,720]{1,0:T(8,128)(2,1)S(1)} collective-permute-done((bf16[32,720]{1,0:T(8,128)(2,1)S(1)}, bf16[32,720]{1,0:T(8,128)(2,1)S(1)}, u32[]{:S(2)}, u32[]{:S(2)}) %collective-permute-start.16) | collective-permute-done | bytes 46112 | tf_op jit(solution)/shard_map/ppermute | solution.py:551
  51.0 1.0 %collective-permute-done.15 = bf16[32,720]{1,0:T(8,128)(2,1)S(1)} collective-permute-done((bf16[32,720]{1,0:T(8,128)(2,1)S(1)}, bf16[32,720]{1,0:T(8,128)(2,1)S(1)}, u32[]{:S(2)}, u32[]{:S(2)}) %collective-permute-start.15) | collective-permute-done | bytes 46112 | tf_op jit(solution)/shard_map/ppermute | solution.py:551
  52.0 0.6 %add_convert_fusion.1 = bf16[32,720]{1,0:T(8,128)(2,1)} fusion(bf16[32,720]{1,0:T(8,128)(2,1)S(1)} %collective-permute-done.16, bf16[32,720]{1,0:T(8,128)(2,1)S(1)} %collective-permute-done.15, f32[32,720]{1,0:T(8,128)S(1)} %get-tuple-element.38, bf16[32,720]{1,0:T(8,128)(2,1)S(1)} %collective-permute-done.14), kind=kLoop, calls=%fused_computation.8 | loop fusion | flops 161280 | bytes 276480 | tf_op jit(solution)/shard_map/convert_element_type | solution.py:604
  (31 shorter events, 2.5 us)
Async XLA Ops:
  4.6 7.7 %copy-start.3 = (bf16[32,720]{1,0:T(8,128)(2,1)S(1)}, bf16[32,720]{1,0:T(8,128)(2,1)}, u32[]{:S(2)}) copy-start(bf16[32,720]{1,0:T(8,128)(2,1)} %rest_3_.1) | copy-start | bytes 138244
  4.6 7.7 %copy-start.4 = (bf16[720,8]{0,1:T(8,128)(2,1)S(1)}, bf16[720,8]{0,1:T(8,128)(2,1)}, u32[]{:S(2)}) copy-start(bf16[720,8]{0,1:T(8,128)(2,1)} %param.25) | copy-start | bytes 34564
  4.6 7.7 %copy-start.5 = (s32[32,4]{0,1:T(4,128)S(1)}, s32[32,4]{0,1:T(4,128)}, u32[]{:S(2)}) copy-start(s32[32,4]{0,1:T(4,128)} %param.26) | copy-start | bytes 1540
  5.5 3.9 %collective-permute-start = (bf16[32,720]{1,0:T(8,128)(2,1)S(1)}, bf16[32,720]{1,0:T(8,128)(2,1)S(1)}, u32[]{:S(2)}, u32[]{:S(2)}) collective-permute-start(bf16[32,720]{1,0:T(8,128)(2,1)S(1)} %get-tuple-element.25), channel_id=1, source_target_pairs={{0,1},{1,0},{2,3},{3,2},{4,5},{5,4},{6,7},{7,6},{8,9},{9,8},{10,11... | collective-permute-start | bytes 138248 | tf_op jit(solution)/shard_map/ppermute | solution.py:544
  6.0 4.9 %collective-permute-start.1 = (bf16[32,720]{1,0:T(8,128)(2,1)S(1)}, bf16[32,720]{1,0:T(8,128)(2,1)S(1)}, u32[]{:S(2)}, u32[]{:S(2)}) collective-permute-start(bf16[32,720]{1,0:T(8,128)(2,1)S(1)} %get-tuple-element.26), channel_id=1, source_target_pairs={{0,16},{1,17},{2,18},{3,19},{4,20},{5,21},{6,22},{7,23},{8,24},{9,... | collective-permute-start | bytes 138248 | tf_op jit(solution)/shard_map/ppermute | solution.py:544
  8.6 3.7 %collective-permute-start.2 = (bf16[32,720]{1,0:T(8,128)(2,1)S(1)}, bf16[32,720]{1,0:T(8,128)(2,1)S(1)}, u32[]{:S(2)}, u32[]{:S(2)}) collective-permute-start(bf16[32,720]{1,0:T(8,128)(2,1)S(1)} %get-tuple-element.27), channel_id=1, source_target_pairs={{0,17},{1,16},{2,19},{3,18},{4,21},{5,20},{6,23},{7,22},{8,25},{9,... | collective-permute-start | bytes 138248 | tf_op jit(solution)/shard_map/ppermute | solution.py:544
  12.3 18.6 %copy-start.1 = (bf16[1,2880,360]{1,2,0:T(8,128)(2,1)S(1)}, bf16[1,2880,360]{1,2,0:T(8,128)(2,1)}, u32[]{:S(2)}) copy-start(bf16[1,2880,360]{1,2,0:T(8,128)(2,1)} %param.27) | copy-start | bytes 6220804
  12.3 18.6 %copy-start.2 = (bf16[1,2880,360]{1,2,0:T(8,128)(2,1)S(1)}, bf16[1,2880,360]{1,2,0:T(8,128)(2,1)}, u32[]{:S(2)}) copy-start(bf16[1,2880,360]{1,2,0:T(8,128)(2,1)} %param.28) | copy-start | bytes 6220804
  12.7 4.5 %collective-permute-start.3 = (bf16[32,768]{1,0:T(8,128)(2,1)S(1)}, bf16[32,768]{1,0:T(8,128)(2,1)S(1)}, u32[]{:S(2)}, u32[]{:S(2)}) collective-permute-start(bf16[32,768]{1,0:T(8,128)(2,1)S(1)} %get-tuple-element.29.rest_0_), channel_id=1, source_target_pairs={{0,4},{1,5},{2,6},{3,7},{4,0},{5,1},{6,2},{7,3},{8,12},{9,13},{10,... | collective-permute-start | bytes 147464 | tf_op jit(solution)/shard_map/ppermute | solution.py:551
  14.3 5.9 %collective-permute-start.4 = (bf16[32,768]{1,0:T(8,128)(2,1)S(1)}, bf16[32,768]{1,0:T(8,128)(2,1)S(1)}, u32[]{:S(2)}, u32[]{:S(2)}) collective-permute-start(bf16[32,768]{1,0:T(8,128)(2,1)S(1)} %get-tuple-element.29.rest_0_), channel_id=1, source_target_pairs={{0,8},{1,9},{2,10},{3,11},{4,12},{5,13},{6,14},{7,15},{8,0},{9,1},... | collective-permute-start | bytes 147464 | tf_op jit(solution)/shard_map/ppermute | solution.py:551
  16.9 5.9 %collective-permute-start.5 = (bf16[32,768]{1,0:T(8,128)(2,1)S(1)}, bf16[32,768]{1,0:T(8,128)(2,1)S(1)}, u32[]{:S(2)}, u32[]{:S(2)}) collective-permute-start(bf16[32,768]{1,0:T(8,128)(2,1)S(1)} %get-tuple-element.29.rest_0_), channel_id=1, source_target_pairs={{0,12},{1,13},{2,14},{3,15},{4,8},{5,9},{6,10},{7,11},{8,4},{9,5},... | collective-permute-start | bytes 147464 | tf_op jit(solution)/shard_map/ppermute | solution.py:551
  23.2 5.6 %collective-permute-start.6 = (bf16[72,768]{1,0:T(8,128)(2,1)S(1)}, bf16[72,768]{1,0:T(8,128)(2,1)S(1)}, u32[]{:S(2)}, u32[]{:S(2)}) collective-permute-start(bf16[72,768]{1,0:T(8,128)(2,1)S(1)} %get-tuple-element.31), channel_id=1, source_target_pairs={{0,2},{1,3},{2,0},{3,1},{4,6},{5,7},{6,4},{7,5},{8,10},{9,11},{10,... | collective-permute-start | bytes 331784 | tf_op jit(solution)/shard_map/ppermute | solution.py:544
  24.8 5.6 %collective-permute-start.8 = (bf16[72,768]{1,0:T(8,128)(2,1)S(1)}, bf16[72,768]{1,0:T(8,128)(2,1)S(1)}, u32[]{:S(2)}, u32[]{:S(2)}) collective-permute-start(bf16[72,768]{1,0:T(8,128)(2,1)S(1)} %get-tuple-element.31), channel_id=1, source_target_pairs={{0,18},{1,19},{2,16},{3,17},{4,22},{5,23},{6,20},{7,21},{8,26},{9,... | collective-permute-start | bytes 331784 | tf_op jit(solution)/shard_map/ppermute | solution.py:544
  25.7 5.0 %collective-permute-start.7 = (bf16[72,768]{1,0:T(8,128)(2,1)S(1)}, bf16[72,768]{1,0:T(8,128)(2,1)S(1)}, u32[]{:S(2)}, u32[]{:S(2)}) collective-permute-start(bf16[72,768]{1,0:T(8,128)(2,1)S(1)} %get-tuple-element.30), channel_id=1, source_target_pairs={{0,16},{1,17},{2,18},{3,19},{4,20},{5,21},{6,22},{7,23},{8,24},{9,... | collective-permute-start | bytes 331784 | tf_op jit(solution)/shard_map/ppermute | solution.py:544
  30.8 1.9 %collective-permute-start.9 = (bf16[2,144,768]{2,1,0:T(8,128)(2,1)S(1)}, bf16[2,144,768]{2,1,0:T(8,128)(2,1)S(1)}, u32[]{:S(2)}, u32[]{:S(2)}) collective-permute-start(bf16[2,144,768]{2,1,0:T(8,128)(2,1)S(1)} %pad_maximum_fusion.own_ref), channel_id=1, source_target_pairs={{0,1},{1,0},{2,3},{3,2},{4,5},{5,4},{6,7},{7,6},{8,9},{9,8},{10,11... | collective-permute-start | bytes 1327112 | tf_op jit(solution)/shard_map/ppermute | solution.py:544
  30.9 1.8 %copy-start = (bf16[1,360,2880]{2,1,0:T(8,128)(2,1)S(1)}, bf16[1,360,2880]{2,1,0:T(8,128)(2,1)}, u32[]{:S(2)}) copy-start(bf16[1,360,2880]{2,1,0:T(8,128)(2,1)} %down_ref.3) | copy-start | bytes 6220804
  34.2 1.9 %collective-permute-start.10 = (bf16[2,144,720]{2,1,0:T(8,128)(2,1)S(1)}, bf16[2,144,720]{2,1,0:T(8,128)(2,1)S(1)}, u32[]{:S(2)}, u32[]{:S(2)}) collective-permute-start(bf16[2,144,720]{2,1,0:T(8,128)(2,1)S(1)} %get-tuple-element.35), channel_id=1, source_target_pairs={{0,1},{1,0},{2,3},{3,2},{4,5},{5,4},{6,7},{7,6},{8,9},{9,8},{10,11... | collective-permute-start | bytes 1244168 | tf_op jit(solution)/shard_map/ppermute | solution.py:544
  36.2 5.7 %collective-permute-start.11 = (bf16[72,720]{1,0:T(8,128)(2,1)S(1)}, bf16[72,720]{1,0:T(8,128)(2,1)S(1)}, u32[]{:S(2)}, u32[]{:S(2)}) collective-permute-start(bf16[72,720]{1,0:T(8,128)(2,1)S(1)} %get-tuple-element.44), channel_id=1, source_target_pairs={{0,16},{1,17},{2,18},{3,19},{4,20},{5,21},{6,22},{7,23},{8,24},{9,... | collective-permute-start | bytes 311048 | tf_op jit(solution)/shard_map/ppermute | solution.py:544
  37.2 6.3 %collective-permute-start.12 = (bf16[72,720]{1,0:T(8,128)(2,1)S(1)}, bf16[72,720]{1,0:T(8,128)(2,1)S(1)}, u32[]{:S(2)}, u32[]{:S(2)}) collective-permute-start(bf16[72,720]{1,0:T(8,128)(2,1)S(1)} %get-tuple-element.43), channel_id=1, source_target_pairs={{0,2},{1,3},{2,0},{3,1},{4,6},{5,7},{6,4},{7,5},{8,10},{9,11},{10,... | collective-permute-start | bytes 311048 | tf_op jit(solution)/shard_map/ppermute | solution.py:544
  38.7 6.0 %collective-permute-start.13 = (bf16[72,720]{1,0:T(8,128)(2,1)S(1)}, bf16[72,720]{1,0:T(8,128)(2,1)S(1)}, u32[]{:S(2)}, u32[]{:S(2)}) collective-permute-start(bf16[72,720]{1,0:T(8,128)(2,1)S(1)} %get-tuple-element.42), channel_id=1, source_target_pairs={{0,18},{1,19},{2,16},{3,17},{4,22},{5,23},{6,20},{7,21},{8,26},{9,... | collective-permute-start | bytes 311048 | tf_op jit(solution)/shard_map/ppermute | solution.py:544
  45.0 6.0 %collective-permute-start.16 = (bf16[32,720]{1,0:T(8,128)(2,1)S(1)}, bf16[32,720]{1,0:T(8,128)(2,1)S(1)}, u32[]{:S(2)}, u32[]{:S(2)}) collective-permute-start(bf16[32,720]{1,0:T(8,128)(2,1)S(1)} %get-tuple-element.41), channel_id=1, source_target_pairs={{0,12},{1,13},{2,14},{3,15},{4,8},{5,9},{6,10},{7,11},{8,4},{9,5},... | collective-permute-start | bytes 138248 | tf_op jit(solution)/shard_map/ppermute | solution.py:551
  46.1 5.9 %collective-permute-start.15 = (bf16[32,720]{1,0:T(8,128)(2,1)S(1)}, bf16[32,720]{1,0:T(8,128)(2,1)S(1)}, u32[]{:S(2)}, u32[]{:S(2)}) collective-permute-start(bf16[32,720]{1,0:T(8,128)(2,1)S(1)} %get-tuple-element.40), channel_id=1, source_target_pairs={{0,8},{1,9},{2,10},{3,11},{4,12},{5,13},{6,14},{7,15},{8,0},{9,1},... | collective-permute-start | bytes 138248 | tf_op jit(solution)/shard_map/ppermute | solution.py:551
  46.1 5.9 %collective-permute-start.14 = (bf16[32,720]{1,0:T(8,128)(2,1)S(1)}, bf16[32,720]{1,0:T(8,128)(2,1)S(1)}, u32[]{:S(2)}, u32[]{:S(2)}) collective-permute-start(bf16[32,720]{1,0:T(8,128)(2,1)S(1)} %get-tuple-element.39), channel_id=1, source_target_pairs={{0,4},{1,5},{2,6},{3,7},{4,0},{5,1},{6,2},{7,3},{8,12},{9,13},{10,... | collective-permute-start | bytes 138248 | tf_op jit(solution)/shard_map/ppermute | solution.py:551
where the time goes:
time: 52.9 us; the launch traced here: 52.7 us
  waiting for transfers between devices  21.4 us (40%)
  starting transfers between devices  19.3 us (36%)
  Pallas kernels  8.85 us (17%)
  other arithmetic  1.47 us (3%)
  local copies, waits for them, and re-layouts  0.85 us (2%)
  between operations  0.81 us (2%)
    ppermute x11, waiting for transfers between devices, send(): lax.ppermute(x, names, swap_table(mesh, lambda g: g ^ near, role, tp))  13.8 us
    ppermute x11, starting transfers between devices, send(): lax.ppermute(x, names, swap_table(mesh, lambda g: g ^ near, role, tp))  10.4 us
    ppermute x6, starting transfers between devices, send_far(): return lax.ppermute(x, names, swap_table(mesh, grp_of, 0, 0))  8.9 us
    ppermute x6, waiting for transfers between devices, send_far(): return lax.ppermute(x, names, swap_table(mesh, grp_of, 0, 0))  7.6 us
    pallas_call x1, Pallas kernels, attend_project(): pl.pallas_call(functools.partial(attend_kernel, grouped=HEADS // KV_HEADS...  3.93 us
    pallas_call x1, Pallas kernels, run_second(): pl.pallas_call(functools.partial(second_kernel, quarter=quarter, topk=top...  1.59 us
  transfers between devices with their start and end apart: 17, of which 14 were waited for; matrix products, arithmetic and copies ran while one was open for 3% of the time, Pallas kernels for 3%

commit v1 on v0

--- a/solution.py
+++ b/solution.py
@@ -356,6 +356,30 @@
     )(activated, w_down)
 
 
+def join_kernel(kept_ref, returned_ref, *outs, n_near):
+    _, items, _ = kept_ref.shape
+    step = items // n_near
+    for n, out in enumerate(outs):
+        at = pl.ds(n % n_near * step, step)
+        total = kept_ref[n // n_near, at].astype(jnp.float32)
+        total = total + returned_ref[n // n_near, at].astype(jnp.float32)
+        out[...] = total.astype(out.dtype)
+
+
+def run_join(kept, returned, n_near):
+    n_role, items, quarter = kept.shape
+    vmem = pl.BlockSpec(memory_space=pltpu.VMEM)
+    n_outs = n_role * n_near
+    return pl.pallas_call(
+        functools.partial(join_kernel, n_near=n_near),
+        in_specs=[vmem, vmem],
+        out_specs=[vmem] * n_outs,
+        out_shape=[jax.ShapeDtypeStruct((items // n_near, quarter), kept.dtype)] * n_outs,
+        compiler_params=pltpu.CompilerParams(vmem_limit_bytes=8 << 20),
+        name="join",
+    )(kept, returned)
+
+
 def three_parts(x):
     high = x.astype(jnp.bfloat16).astype(jnp.float32)
     rest = x - high
@@ -588,12 +612,11 @@
         )
         returned = send(sent, tp=1)
         kept = run_third(activated, w_down, n_role, quarter, n_tp)
-        acc = kept.astype(jnp.float32) + returned.astype(jnp.float32)
-        acc = acc.astype(jnp.bfloat16).reshape(n_role, n_near, n_far * cap, quarter)
+        acc = run_join(kept, returned, n_near)
         back = []
         for j in range(n_near):
             for i in range(n_role):
-                piece = acc[i, j]
+                piece = acc[i * n_near + j]
                 if (j, i) != (0, 0):
                     piece = send(piece, near=j, role=i)
                 back.append(piece)

time: 52.9 us -> 52.8 us (level)
  no operation moved by 1% of the time
where the time goes in v1:
time: 52.8 us; the launch traced here: 52.6 us
  waiting for transfers between devices  21.4 us (41%)
  starting transfers between devices  19.3 us (37%)
  Pallas kernels  8.96 us (17%)
  other arithmetic  1.35 us (3%)
  local copies, waits for them, and re-layouts  0.81 us (2%)
  between operations  0.8 us (2%)
    ppermute x11, waiting for transfers between devices, send(): lax.ppermute(x, names, swap_table(mesh, lambda g: g ^ near, role, tp))  13.8 us
    ppermute x11, starting transfers between devices, send(): lax.ppermute(x, names, swap_table(mesh, lambda g: g ^ near, role, tp))  10.4 us
    ppermute x6, starting transfers between devices, send_far(): return lax.ppermute(x, names, swap_table(mesh, grp_of, 0, 0))  8.9 us
    ppermute x6, waiting for transfers between devices, send_far(): return lax.ppermute(x, names, swap_table(mesh, grp_of, 0, 0))  7.6 us
    pallas_call x1, Pallas kernels, attend_project(): pl.pallas_call(functools.partial(attend_kernel, grouped=HEADS // KV_HEADS...  3.93 us
    pallas_call x1, Pallas kernels, run_second(): pl.pallas_call(functools.partial(second_kernel, quarter=quarter, topk=top...  1.59 us
  transfers between devices with their start and end apart: 17, of which 14 were waited for; matrix products, arithmetic and copies ran while one was open for 3% of the time, Pallas kernels for 3%

profile of v1, /device:TPU:0, one launch (start us, length us, event | category | flops | bytes accessed | tf_op | source)
XLA Modules:
  0.0 52.6 jit_solution(2065703712872275781)
XLA Ops:
  0.6 3.9 %attend_project.1 = (bf16[32,720]{1,0:T(8,128)(2,1)S(1)}, bf16[32,720]{1,0:T(8,128)(2,1)S(1)}, bf16[32,1024]{1,0:T(8,128)(2,1)S(1)}, bf16[2,720,1024]{2,1,0:T(8,128)(2,1)S(1)}) custom-call(s32[32]{0:T(128)} %len_hbm.1, s32[32]{0:T(128)} %start_hbm.1, bf16[32,1024]{1,0:T(8,128)(2,1)} %q_hbm.1, bf16[32,128]{1,0:T(8,128)(2,1)} %kn_hbm.1, ...), custom_call_target="tpu_custom_call" | custom-call | tf_op jit(solution)/shard_map/attend_project/pallas_call | solution.py:164
  4.6 0.9 %project.1 = (f32[32,720]{1,0:T(8,128)S(1)}, bf16[32,720]{1,0:T(8,128)(2,1)S(1)}) custom-call(bf16[32,1024]{1,0:T(8,128)(2,1)S(1)} %get-tuple-element.26.stacked_ref, bf16[2,720,1024]{2,1,0:T(8,128)(2,1)S(1)} %get-tuple-element.27.later_ref), custom_call_target="tpu_custom_call" | custom-call | tf_op jit(solution)/shard_map/project/pallas_call | solution.py:205
  5.5 0.5 collective-permute-start
  6.0 2.5 %collective-permute-start.1 = (bf16[32,720]{1,0:T(8,128)(2,1)S(1)}, bf16[32,720]{1,0:T(8,128)(2,1)S(1)}, u32[]{:S(2)}, u32[]{:S(2)}) collective-permute-start(bf16[32,720]{1,0:T(8,128)(2,1)S(1)} %get-tuple-element.30), channel_id=1, source_target_pairs={{0,16},{1,17},{2,18},{3,19},{4,20},{5,21},{6,22},{7,23},{8,24},{9,... | collective-permute-start | bytes 138248 | tf_op jit(solution)/shard_map/ppermute | solution.py:568
  8.6 0.8 %dynamic_slice.3 = f32[720]{0:T(1024)S(1)} dynamic-slice(f32[2880]{0:T(1024)} %param.24, s32[]{:T(128)S(6)} %select_n.3), dynamic_slice_sizes={720} | dynamic-slice | bytes 5764 | tf_op jit(solution)/shard_map/dynamic_slice | solution.py:594
  9.4 1.5 %collective-permute-done.1.rest_1_ = bf16[32,720]{1,0:T(8,128)(2,1)S(1)} collective-permute-done((bf16[32,720]{1,0:T(8,128)(2,1)S(1)}, bf16[32,720]{1,0:T(8,128)(2,1)S(1)}, u32[]{:S(2)}, u32[]{:S(2)}) %collective-permute-start.1) | collective-permute-done | bytes 46112 | tf_op jit(solution)/shard_map/ppermute | solution.py:568
  10.9 1.4 %collective-permute-done.2.rest_2_ = bf16[32,720]{1,0:T(8,128)(2,1)S(1)} collective-permute-done((bf16[32,720]{1,0:T(8,128)(2,1)S(1)}, bf16[32,720]{1,0:T(8,128)(2,1)S(1)}, u32[]{:S(2)}, u32[]{:S(2)}) %collective-permute-start.2) | collective-permute-done | bytes 46112 | tf_op jit(solution)/shard_map/ppermute | solution.py:568
  12.7 1.6 %collective-permute-start.3 = (bf16[32,768]{1,0:T(8,128)(2,1)S(1)}, bf16[32,768]{1,0:T(8,128)(2,1)S(1)}, u32[]{:S(2)}, u32[]{:S(2)}) collective-permute-start(bf16[32,768]{1,0:T(8,128)(2,1)S(1)} %get-tuple-element.33.rest_0_), channel_id=1, source_target_pairs={{0,4},{1,5},{2,6},{3,7},{4,0},{5,1},{6,2},{7,3},{8,12},{9,13},{10,... | collective-permute-start | bytes 147464 | tf_op jit(solution)/shard_map/ppermute | solution.py:575
  14.3 2.6 %collective-permute-start.4 = (bf16[32,768]{1,0:T(8,128)(2,1)S(1)}, bf16[32,768]{1,0:T(8,128)(2,1)S(1)}, u32[]{:S(2)}, u32[]{:S(2)}) collective-permute-start(bf16[32,768]{1,0:T(8,128)(2,1)S(1)} %get-tuple-element.33.rest_0_), channel_id=1, source_target_pairs={{0,8},{1,9},{2,10},{3,11},{4,12},{5,13},{6,14},{7,15},{8,0},{9,1},... | collective-permute-start | bytes 147464 | tf_op jit(solution)/shard_map/ppermute | solution.py:575
  17.1 3.1 %collective-permute-done.4.rest_2_ = bf16[32,768]{1,0:T(8,128)(2,1)S(1)} collective-permute-done((bf16[32,768]{1,0:T(8,128)(2,1)S(1)}, bf16[32,768]{1,0:T(8,128)(2,1)S(1)}, u32[]{:S(2)}, u32[]{:S(2)}) %collective-permute-start.4) | collective-permute-done | bytes 49184 | tf_op jit(solution)/shard_map/ppermute | solution.py:575
  20.2 2.6 %collective-permute-done.5.rest_3_ = bf16[32,768]{1,0:T(8,128)(2,1)S(1)} collective-permute-done((bf16[32,768]{1,0:T(8,128)(2,1)S(1)}, bf16[32,768]{1,0:T(8,128)(2,1)S(1)}, u32[]{:S(2)}, u32[]{:S(2)}) %collective-permute-start.5) | collective-permute-done | bytes 49184 | tf_op jit(solution)/shard_map/ppermute | solution.py:575
  23.2 1.6 %collective-permute-start.6 = (bf16[72,768]{1,0:T(8,128)(2,1)S(1)}, bf16[72,768]{1,0:T(8,128)(2,1)S(1)}, u32[]{:S(2)}, u32[]{:S(2)}) collective-permute-start(bf16[72,768]{1,0:T(8,128)(2,1)S(1)} %get-tuple-element.35), channel_id=1, source_target_pairs={{0,2},{1,3},{2,0},{3,1},{4,6},{5,7},{6,4},{7,5},{8,10},{9,11},{10,... | collective-permute-start | bytes 331784 | tf_op jit(solution)/shard_map/ppermute | solution.py:568
  24.8 0.9 %collective-permute-start.8 = (bf16[72,768]{1,0:T(8,128)(2,1)S(1)}, bf16[72,768]{1,0:T(8,128)(2,1)S(1)}, u32[]{:S(2)}, u32[]{:S(2)}) collective-permute-start(bf16[72,768]{1,0:T(8,128)(2,1)S(1)} %get-tuple-element.35), channel_id=1, source_target_pairs={{0,18},{1,19},{2,16},{3,17},{4,22},{5,23},{6,20},{7,21},{8,26},{9,... | collective-permute-start | bytes 331784 | tf_op jit(solution)/shard_map/ppermute | solution.py:568
  25.7 1.1 %collective-permute-start.7 = (bf16[72,768]{1,0:T(8,128)(2,1)S(1)}, bf16[72,768]{1,0:T(8,128)(2,1)S(1)}, u32[]{:S(2)}, u32[]{:S(2)}) collective-permute-start(bf16[72,768]{1,0:T(8,128)(2,1)S(1)} %get-tuple-element.34), channel_id=1, source_target_pairs={{0,16},{1,17},{2,18},{3,19},{4,20},{5,21},{6,22},{7,23},{8,24},{9,... | collective-permute-start | bytes 331784 | tf_op jit(solution)/shard_map/ppermute | solution.py:568
  26.8 2.1 %collective-permute-done.6 = bf16[72,768]{1,0:T(8,128)(2,1)S(1)} collective-permute-done((bf16[72,768]{1,0:T(8,128)(2,1)S(1)}, bf16[72,768]{1,0:T(8,128)(2,1)S(1)}, u32[]{:S(2)}, u32[]{:S(2)}) %collective-permute-start.6) | collective-permute-done | bytes 110624 | tf_op jit(solution)/shard_map/ppermute | solution.py:568
  28.9 1.6 %collective-permute-done.8 = bf16[72,768]{1,0:T(8,128)(2,1)S(1)} collective-permute-done((bf16[72,768]{1,0:T(8,128)(2,1)S(1)}, bf16[72,768]{1,0:T(8,128)(2,1)S(1)}, u32[]{:S(2)}, u32[]{:S(2)}) %collective-permute-start.8) | collective-permute-done | bytes 110624 | tf_op jit(solution)/shard_map/ppermute | solution.py:568
  30.9 0.9 %expert_first.1 = (f32[144,360]{1,0:T(8,128)S(1)}, f32[144,360]{1,0:T(8,128)S(1)}) custom-call(bf16[2,144,768]{2,1,0:T(8,128)(2,1)S(1)} %pad_maximum_fusion.own_ref, bf16[1,360,2880]{2,1,0:T(8,128)(2,1)S(1)} %bitcast.9, bf16[1,360,2880]{2,1,0:T(8,128)(2,1)S(1)} %bitcast.11), custom_call_target="tpu_custom_call" | custom-call | tf_op jit(solution)/shard_map/expert_first/pallas_call | solution.py:320
  31.8 0.8 %collective-permute-done.9.other_ref = bf16[2,144,768]{2,1,0:T(8,128)(2,1)S(1)} collective-permute-done((bf16[2,144,768]{2,1,0:T(8,128)(2,1)S(1)}, bf16[2,144,768]{2,1,0:T(8,128)(2,1)S(1)}, u32[]{:S(2)}, u32[]{:S(2)}) %collective-permute-start.9) | collective-permute-done | bytes 442400 | tf_op jit(solution)/shard_map/ppermute | solution.py:568
  32.6 1.6 %expert_second.1 = (bf16[2,144,720]{2,1,0:T(8,128)(2,1)S(1)}, bf16[144,360]{1,0:T(8,128)(2,1)S(1)}) custom-call(bf16[2,144,768]{2,1,0:T(8,128)(2,1)S(1)} %pad_maximum_fusion.own_ref, bf16[2,144,768]{2,1,0:T(8,128)(2,1)S(1)} %collective-permute-done.9.other_ref, f32[144,360]{1,0:T(8,128)S(1)} %get-tuple-element.36.gate_in, ...), custom_call_target="tpu_custom_call" | custom-call | tf_op jit(solution)/shard_map/expert_second/pallas_call | solution.py:333
  34.9 1.2 %collective-permute-done.10.returned_ref = bf16[2,144,720]{2,1,0:T(8,128)(2,1)S(1)} collective-permute-done((bf16[2,144,720]{2,1,0:T(8,128)(2,1)S(1)}, bf16[2,144,720]{2,1,0:T(8,128)(2,1)S(1)}, u32[]{:S(2)}, u32[]{:S(2)}) %collective-permute-start.10) | collective-permute-done | bytes 414752 | tf_op jit(solution)/shard_map/ppermute | solution.py:568
  36.2 1.0 %collective-permute-start.11 = (bf16[72,720]{1,0:T(8,128)(2,1)S(1)}, bf16[72,720]{1,0:T(8,128)(2,1)S(1)}, u32[]{:S(2)}, u32[]{:S(2)}) collective-permute-start(bf16[72,720]{1,0:T(8,128)(2,1)S(1)} %get-tuple-element.41), channel_id=1, source_target_pairs={{0,16},{1,17},{2,18},{3,19},{4,20},{5,21},{6,22},{7,23},{8,24},{9,... | collective-permute-start | bytes 311048 | tf_op jit(solution)/shard_map/ppermute | solution.py:568
  37.2 1.5 %collective-permute-start.12 = (bf16[72,720]{1,0:T(8,128)(2,1)S(1)}, bf16[72,720]{1,0:T(8,128)(2,1)S(1)}, u32[]{:S(2)}, u32[]{:S(2)}) collective-permute-start(bf16[72,720]{1,0:T(8,128)(2,1)S(1)} %get-tuple-element.42), channel_id=1, source_target_pairs={{0,2},{1,3},{2,0},{3,1},{4,6},{5,7},{6,4},{7,5},{8,10},{9,11},{10,... | collective-permute-start | bytes 311048 | tf_op jit(solution)/shard_map/ppermute | solution.py:568
  38.7 1.0 %collective-permute-start.13 = (bf16[72,720]{1,0:T(8,128)(2,1)S(1)}, bf16[72,720]{1,0:T(8,128)(2,1)S(1)}, u32[]{:S(2)}, u32[]{:S(2)}) collective-permute-start(bf16[72,720]{1,0:T(8,128)(2,1)S(1)} %get-tuple-element.43), channel_id=1, source_target_pairs={{0,18},{1,19},{2,16},{3,17},{4,22},{5,23},{6,20},{7,21},{8,26},{9,... | collective-permute-start | bytes 311048 | tf_op jit(solution)/shard_map/ppermute | solution.py:568
  39.7 2.1 %collective-permute-done.11.refs_1_ = bf16[72,720]{1,0:T(8,128)(2,1)S(1)} collective-permute-done((bf16[72,720]{1,0:T(8,128)(2,1)S(1)}, bf16[72,720]{1,0:T(8,128)(2,1)S(1)}, u32[]{:S(2)}, u32[]{:S(2)}) %collective-permute-start.11) | collective-permute-done | bytes 103712 | tf_op jit(solution)/shard_map/ppermute | solution.py:568
  41.9 1.5 %collective-permute-done.12.refs_2_ = bf16[72,720]{1,0:T(8,128)(2,1)S(1)} collective-permute-done((bf16[72,720]{1,0:T(8,128)(2,1)S(1)}, bf16[72,720]{1,0:T(8,128)(2,1)S(1)}, u32[]{:S(2)}, u32[]{:S(2)}) %collective-permute-start.12) | collective-permute-done | bytes 103712 | tf_op jit(solution)/shard_map/ppermute | solution.py:568
  43.4 1.2 %collective-permute-done.13.refs_3_ = bf16[72,720]{1,0:T(8,128)(2,1)S(1)} collective-permute-done((bf16[72,720]{1,0:T(8,128)(2,1)S(1)}, bf16[72,720]{1,0:T(8,128)(2,1)S(1)}, u32[]{:S(2)}, u32[]{:S(2)}) %collective-permute-start.13) | collective-permute-done | bytes 103712 | tf_op jit(solution)/shard_map/ppermute | solution.py:568
  45.0 1.1 %collective-permute-start.16 = (bf16[32,720]{1,0:T(8,128)(2,1)S(1)}, bf16[32,720]{1,0:T(8,128)(2,1)S(1)}, u32[]{:S(2)}, u32[]{:S(2)}) collective-permute-start(bf16[32,720]{1,0:T(8,128)(2,1)S(1)} %get-tuple-element.49), channel_id=1, source_target_pairs={{0,12},{1,13},{2,14},{3,15},{4,8},{5,9},{6,10},{7,11},{8,4},{9,5},... | collective-permute-start | bytes 138248 | tf_op jit(solution)/shard_map/ppermute | solution.py:575
  46.1 3.3 %collective-permute-start.14 = (bf16[32,720]{1,0:T(8,128)(2,1)S(1)}, bf16[32,720]{1,0:T(8,128)(2,1)S(1)}, u32[]{:S(2)}, u32[]{:S(2)}) collective-permute-start(bf16[32,720]{1,0:T(8,128)(2,1)S(1)} %get-tuple-element.47), channel_id=1, source_target_pairs={{0,4},{1,5},{2,6},{3,7},{4,0},{5,1},{6,2},{7,3},{8,12},{9,13},{10,... | collective-permute-start | bytes 138248 | tf_op jit(solution)/shard_map/ppermute | solution.py:575
  49.4 0.6 %convert_element_type.15 = bf16[32,720]{1,0:T(8,128)(2,1)} convert(f32[32,720]{1,0:T(8,128)S(1)} %get-tuple-element.32) | non-fusion elementwise | flops 23040 | bytes 138240 | tf_op jit(solution)/shard_map/convert_element_type | solution.py:597
  50.0 0.9 %collective-permute-done.16 = bf16[32,720]{1,0:T(8,128)(2,1)S(1)} collective-permute-done((bf16[32,720]{1,0:T(8,128)(2,1)S(1)}, bf16[32,720]{1,0:T(8,128)(2,1)S(1)}, u32[]{:S(2)}, u32[]{:S(2)}) %collective-permute-start.16) | collective-permute-done | bytes 46112 | tf_op jit(solution)/shard_map/ppermute | solution.py:575
  51.0 1.0 %collective-permute-done.15 = bf16[32,720]{1,0:T(8,128)(2,1)S(1)} collective-permute-done((bf16[32,720]{1,0:T(8,128)(2,1)S(1)}, bf16[32,720]{1,0:T(8,128)(2,1)S(1)}, u32[]{:S(2)}, u32[]{:S(2)}) %collective-permute-start.15) | collective-permute-done | bytes 46112 | tf_op jit(solution)/shard_map/ppermute | solution.py:575
  52.0 0.6 %add_convert_fusion = bf16[32,720]{1,0:T(8,128)(2,1)} fusion(bf16[32,720]{1,0:T(8,128)(2,1)S(1)} %collective-permute-done.16, bf16[32,720]{1,0:T(8,128)(2,1)S(1)} %collective-permute-done.15, f32[32,720]{1,0:T(8,128)S(1)} %get-tuple-element.46, bf16[32,720]{1,0:T(8,128)(2,1)S(1)} %collective-permute-done.14), kind=kLoop, calls=%fused_computation.3 | loop fusion | flops 161280 | bytes 276480 | tf_op jit(solution)/shard_map/convert_element_type | solution.py:627
  (30 shorter events, 2.5 us)
Async XLA Ops:
  4.6 7.7 %copy-start.3 = (bf16[32,720]{1,0:T(8,128)(2,1)S(1)}, bf16[32,720]{1,0:T(8,128)(2,1)}, u32[]{:S(2)}) copy-start(bf16[32,720]{1,0:T(8,128)(2,1)} %rest_3_.1) | copy-start | bytes 138244
  4.6 7.7 %copy-start.4 = (bf16[720,8]{0,1:T(8,128)(2,1)S(1)}, bf16[720,8]{0,1:T(8,128)(2,1)}, u32[]{:S(2)}) copy-start(bf16[720,8]{0,1:T(8,128)(2,1)} %param.25) | copy-start | bytes 34564
  4.6 7.7 %copy-start.5 = (s32[32,4]{0,1:T(4,128)S(1)}, s32[32,4]{0,1:T(4,128)}, u32[]{:S(2)}) copy-start(s32[32,4]{0,1:T(4,128)} %param.26) | copy-start | bytes 1540
  5.5 3.9 %collective-permute-start = (bf16[32,720]{1,0:T(8,128)(2,1)S(1)}, bf16[32,720]{1,0:T(8,128)(2,1)S(1)}, u32[]{:S(2)}, u32[]{:S(2)}) collective-permute-start(bf16[32,720]{1,0:T(8,128)(2,1)S(1)} %get-tuple-element.29), channel_id=1, source_target_pairs={{0,1},{1,0},{2,3},{3,2},{4,5},{5,4},{6,7},{7,6},{8,9},{9,8},{10,11... | collective-permute-start | bytes 138248 | tf_op jit(solution)/shard_map/ppermute | solution.py:568
  6.0 4.9 %collective-permute-start.1 = (bf16[32,720]{1,0:T(8,128)(2,1)S(1)}, bf16[32,720]{1,0:T(8,128)(2,1)S(1)}, u32[]{:S(2)}, u32[]{:S(2)}) collective-permute-start(bf16[32,720]{1,0:T(8,128)(2,1)S(1)} %get-tuple-element.30), channel_id=1, source_target_pairs={{0,16},{1,17},{2,18},{3,19},{4,20},{5,21},{6,22},{7,23},{8,24},{9,... | collective-permute-start | bytes 138248 | tf_op jit(solution)/shard_map/ppermute | solution.py:568
  8.6 3.7 %collective-permute-start.2 = (bf16[32,720]{1,0:T(8,128)(2,1)S(1)}, bf16[32,720]{1,0:T(8,128)(2,1)S(1)}, u32[]{:S(2)}, u32[]{:S(2)}) collective-permute-start(bf16[32,720]{1,0:T(8,128)(2,1)S(1)} %get-tuple-element.31), channel_id=1, source_target_pairs={{0,17},{1,16},{2,19},{3,18},{4,21},{5,20},{6,23},{7,22},{8,25},{9,... | collective-permute-start | bytes 138248 | tf_op jit(solution)/shard_map/ppermute | solution.py:568
  12.3 18.6 %copy-start.1 = (bf16[1,2880,360]{1,2,0:T(8,128)(2,1)S(1)}, bf16[1,2880,360]{1,2,0:T(8,128)(2,1)}, u32[]{:S(2)}) copy-start(bf16[1,2880,360]{1,2,0:T(8,128)(2,1)} %param.27) | copy-start | bytes 6220804
  12.3 18.6 %copy-start.2 = (bf16[1,2880,360]{1,2,0:T(8,128)(2,1)S(1)}, bf16[1,2880,360]{1,2,0:T(8,128)(2,1)}, u32[]{:S(2)}) copy-start(bf16[1,2880,360]{1,2,0:T(8,128)(2,1)} %param.28) | copy-start | bytes 6220804
  12.7 4.5 %collective-permute-start.3 = (bf16[32,768]{1,0:T(8,128)(2,1)S(1)}, bf16[32,768]{1,0:T(8,128)(2,1)S(1)}, u32[]{:S(2)}, u32[]{:S(2)}) collective-permute-start(bf16[32,768]{1,0:T(8,128)(2,1)S(1)} %get-tuple-element.33.rest_0_), channel_id=1, source_target_pairs={{0,4},{1,5},{2,6},{3,7},{4,0},{5,1},{6,2},{7,3},{8,12},{9,13},{10,... | collective-permute-start | bytes 147464 | tf_op jit(solution)/shard_map/ppermute | solution.py:575
  14.3 5.9 %collective-permute-start.4 = (bf16[32,768]{1,0:T(8,128)(2,1)S(1)}, bf16[32,768]{1,0:T(8,128)(2,1)S(1)}, u32[]{:S(2)}, u32[]{:S(2)}) collective-permute-start(bf16[32,768]{1,0:T(8,128)(2,1)S(1)} %get-tuple-element.33.rest_0_), channel_id=1, source_target_pairs={{0,8},{1,9},{2,10},{3,11},{4,12},{5,13},{6,14},{7,15},{8,0},{9,1},... | collective-permute-start | bytes 147464 | tf_op jit(solution)/shard_map/ppermute | solution.py:575
  16.9 5.9 %collective-permute-start.5 = (bf16[32,768]{1,0:T(8,128)(2,1)S(1)}, bf16[32,768]{1,0:T(8,128)(2,1)S(1)}, u32[]{:S(2)}, u32[]{:S(2)}) collective-permute-start(bf16[32,768]{1,0:T(8,128)(2,1)S(1)} %get-tuple-element.33.rest_0_), channel_id=1, source_target_pairs={{0,12},{1,13},{2,14},{3,15},{4,8},{5,9},{6,10},{7,11},{8,4},{9,5},... | collective-permute-start | bytes 147464 | tf_op jit(solution)/shard_map/ppermute | solution.py:575
  23.2 5.6 %collective-permute-start.6 = (bf16[72,768]{1,0:T(8,128)(2,1)S(1)}, bf16[72,768]{1,0:T(8,128)(2,1)S(1)}, u32[]{:S(2)}, u32[]{:S(2)}) collective-permute-start(bf16[72,768]{1,0:T(8,128)(2,1)S(1)} %get-tuple-element.35), channel_id=1, source_target_pairs={{0,2},{1,3},{2,0},{3,1},{4,6},{5,7},{6,4},{7,5},{8,10},{9,11},{10,... | collective-permute-start | bytes 331784 | tf_op jit(solution)/shard_map/ppermute | solution.py:568
  24.8 5.6 %collective-permute-start.8 = (bf16[72,768]{1,0:T(8,128)(2,1)S(1)}, bf16[72,768]{1,0:T(8,128)(2,1)S(1)}, u32[]{:S(2)}, u32[]{:S(2)}) collective-permute-start(bf16[72,768]{1,0:T(8,128)(2,1)S(1)} %get-tuple-element.35), channel_id=1, source_target_pairs={{0,18},{1,19},{2,16},{3,17},{4,22},{5,23},{6,20},{7,21},{8,26},{9,... | collective-permute-start | bytes 331784 | tf_op jit(solution)/shard_map/ppermute | solution.py:568
  25.7 5.0 %collective-permute-start.7 = (bf16[72,768]{1,0:T(8,128)(2,1)S(1)}, bf16[72,768]{1,0:T(8,128)(2,1)S(1)}, u32[]{:S(2)}, u32[]{:S(2)}) collective-permute-start(bf16[72,768]{1,0:T(8,128)(2,1)S(1)} %get-tuple-element.34), channel_id=1, source_target_pairs={{0,16},{1,17},{2,18},{3,19},{4,20},{5,21},{6,22},{7,23},{8,24},{9,... | collective-permute-start | bytes 331784 | tf_op jit(solution)/shard_map/ppermute | solution.py:568
  30.8 1.9 %collective-permute-start.9 = (bf16[2,144,768]{2,1,0:T(8,128)(2,1)S(1)}, bf16[2,144,768]{2,1,0:T(8,128)(2,1)S(1)}, u32[]{:S(2)}, u32[]{:S(2)}) collective-permute-start(bf16[2,144,768]{2,1,0:T(8,128)(2,1)S(1)} %pad_maximum_fusion.own_ref), channel_id=1, source_target_pairs={{0,1},{1,0},{2,3},{3,2},{4,5},{5,4},{6,7},{7,6},{8,9},{9,8},{10,11... | collective-permute-start | bytes 1327112 | tf_op jit(solution)/shard_map/ppermute | solution.py:568
  30.9 1.8 %copy-start = (bf16[1,360,2880]{2,1,0:T(8,128)(2,1)S(1)}, bf16[1,360,2880]{2,1,0:T(8,128)(2,1)}, u32[]{:S(2)}) copy-start(bf16[1,360,2880]{2,1,0:T(8,128)(2,1)} %down_ref.3) | copy-start | bytes 6220804
  34.2 1.9 %collective-permute-start.10 = (bf16[2,144,720]{2,1,0:T(8,128)(2,1)S(1)}, bf16[2,144,720]{2,1,0:T(8,128)(2,1)S(1)}, u32[]{:S(2)}, u32[]{:S(2)}) collective-permute-start(bf16[2,144,720]{2,1,0:T(8,128)(2,1)S(1)} %get-tuple-element.39), channel_id=1, source_target_pairs={{0,1},{1,0},{2,3},{3,2},{4,5},{5,4},{6,7},{7,6},{8,9},{9,8},{10,11... | collective-permute-start | bytes 1244168 | tf_op jit(solution)/shard_map/ppermute | solution.py:568
  36.2 5.7 %collective-permute-start.11 = (bf16[72,720]{1,0:T(8,128)(2,1)S(1)}, bf16[72,720]{1,0:T(8,128)(2,1)S(1)}, u32[]{:S(2)}, u32[]{:S(2)}) collective-permute-start(bf16[72,720]{1,0:T(8,128)(2,1)S(1)} %get-tuple-element.41), channel_id=1, source_target_pairs={{0,16},{1,17},{2,18},{3,19},{4,20},{5,21},{6,22},{7,23},{8,24},{9,... | collective-permute-start | bytes 311048 | tf_op jit(solution)/shard_map/ppermute | solution.py:568
  37.2 6.3 %collective-permute-start.12 = (bf16[72,720]{1,0:T(8,128)(2,1)S(1)}, bf16[72,720]{1,0:T(8,128)(2,1)S(1)}, u32[]{:S(2)}, u32[]{:S(2)}) collective-permute-start(bf16[72,720]{1,0:T(8,128)(2,1)S(1)} %get-tuple-element.42), channel_id=1, source_target_pairs={{0,2},{1,3},{2,0},{3,1},{4,6},{5,7},{6,4},{7,5},{8,10},{9,11},{10,... | collective-permute-start | bytes 311048 | tf_op jit(solution)/shard_map/ppermute | solution.py:568
  38.7 6.0 %collective-permute-start.13 = (bf16[72,720]{1,0:T(8,128)(2,1)S(1)}, bf16[72,720]{1,0:T(8,128)(2,1)S(1)}, u32[]{:S(2)}, u32[]{:S(2)}) collective-permute-start(bf16[72,720]{1,0:T(8,128)(2,1)S(1)} %get-tuple-element.43), channel_id=1, source_target_pairs={{0,18},{1,19},{2,16},{3,17},{4,22},{5,23},{6,20},{7,21},{8,26},{9,... | collective-permute-start | bytes 311048 | tf_op jit(solution)/shard_map/ppermute | solution.py:568
  45.0 6.0 %collective-permute-start.16 = (bf16[32,720]{1,0:T(8,128)(2,1)S(1)}, bf16[32,720]{1,0:T(8,128)(2,1)S(1)}, u32[]{:S(2)}, u32[]{:S(2)}) collective-permute-start(bf16[32,720]{1,0:T(8,128)(2,1)S(1)} %get-tuple-element.49), channel_id=1, source_target_pairs={{0,12},{1,13},{2,14},{3,15},{4,8},{5,9},{6,10},{7,11},{8,4},{9,5},... | collective-permute-start | bytes 138248 | tf_op jit(solution)/shard_map/ppermute | solution.py:575
  46.1 5.9 %collective-permute-start.15 = (bf16[32,720]{1,0:T(8,128)(2,1)S(1)}, bf16[32,720]{1,0:T(8,128)(2,1)S(1)}, u32[]{:S(2)}, u32[]{:S(2)}) collective-permute-start(bf16[32,720]{1,0:T(8,128)(2,1)S(1)} %get-tuple-element.48), channel_id=1, source_target_pairs={{0,8},{1,9},{2,10},{3,11},{4,12},{5,13},{6,14},{7,15},{8,0},{9,1},... | collective-permute-start | bytes 138248 | tf_op jit(solution)/shard_map/ppermute | solution.py:575
  46.1 5.9 %collective-permute-start.14 = (bf16[32,720]{1,0:T(8,128)(2,1)S(1)}, bf16[32,720]{1,0:T(8,128)(2,1)S(1)}, u32[]{:S(2)}, u32[]{:S(2)}) collective-permute-start(bf16[32,720]{1,0:T(8,128)(2,1)S(1)} %get-tuple-element.47), channel_id=1, source_target_pairs={{0,4},{1,5},{2,6},{3,7},{4,0},{5,1},{6,2},{7,3},{8,12},{9,13},{10,... | collective-permute-start | bytes 138248 | tf_op jit(solution)/shard_map/ppermute | solution.py:575
